TPU v7x, 32 devices: a whole 2x2x4 slice. The times are simulated.
32 devices in a mesh: gx: 2 (over x), gy: 4 (over y, core), gz: 4 (over z).
Axes of the slice: x: 2, y: 2, z: 4, core: 2. Of those that a mesh axis runs over, the one named last changes fastest.
Arguments:
- grains: float32 [12, 32, 32, 512], P(None, 'gz', 'gx', 'gy'), may hold values from 0 to 0.6
- solute: float32 [32, 32, 512], P('gz', 'gx', 'gy'), may hold values from 0 to 0.6
- thermal: float32 [4, 2, 4, 20, 4096], P('gz', 'gx', 'gy'), may hold values from 0.5 to 1.5
- block_slot: int32 [4, 2, 4, 20], P('gz', 'gx', 'gy'), may hold values from -1 to 19, as said below
- block_owner: int32 [4, 2, 4, 20], P('gz', 'gx', 'gy'), may hold values from -1 to 3, as said below
- block_offset: int32 [4, 2, 4, 3, 20], P('gz', 'gx', 'gy'), may hold values from -31 to 128, as said below
Outputs:
- grains_out: float32 [12, 32, 32, 512], P(None, 'gz', 'gx', 'gy')
- solute_out: float32 [32, 32, 512], P('gz', 'gx', 'gy')
- temperature: float32 [32, 32, 512], P('gz', 'gx', 'gy')
Inputs may be any that keep to these rules, and one draw needn't show every extreme that they name: `block_slot`: -1 exactly where block_owner is -1; the live entries of all tiles name distinct pairs (owner, slot) within a column. `block_owner`: -1 marks an empty entry. No owner serves more than 5 live entries of one tile; in every draw, in each column, some owner serves 5 entries of every tile of that column; and in every draw some tile of the box has all 20 entries live. `block_offset`: 0 for empty entries. Along each dimension the live starts of a tile differ by multiples of 32, and the hats of a tile's live blocks sum to one at each of its cells.
All inputs are finite; a program needn't handle non-finite values.
Results may differ from a plain program's by a relative error of at most 0.0003.
Values sent between devices are 32-bit elements; how exact they have to be, the bound alone decides.
No kernel may reach another device: no remote copies, remote signals or barrier semaphores. Data moves between devices by JAX's collectives and lax.ppermute only.
A program may use at most 64 MiB of HBM per device.

v0:
```python
import functools

import jax
import jax.numpy as jnp
from jax import lax
from jax.experimental import pallas as pl
from jax.experimental.pallas import tpu as pltpu
from jax.sharding import PartitionSpec as P


NODES = 16
STEPS = 3
LANES = 128
ROWS = 8
FAR = 4096

VMEM = pl.BlockSpec(memory_space=pltpu.VMEM)
HBM = pl.BlockSpec(memory_space=pltpu.HBM)
SMEM = pl.BlockSpec(memory_space=pltpu.SMEM)

PARAMS = pltpu.CompilerParams(vmem_limit_bytes=12 * 1024 * 1024)


def log2(size):
    assert size & (size - 1) == 0
    return size.bit_length() - 1


def half_up(start):
    return (start + (start & 1)) >> 1


def route_kernel(ring, capacity, *refs):
    lists, parity, picks = refs[3 : 3 + ring], refs[3 + ring], refs[4 + ring]
    slot_ref, owner_ref, start_ref, arrivals = refs[5 + ring :]
    copies = [
        pltpu.make_async_copy(source, target, arrivals.at[i])
        for i, (source, target) in enumerate(zip(refs[:3], (slot_ref, owner_ref, start_ref)))
    ]
    for copy in copies:
        copy.start()
    for copy in copies:
        copy.wait()
    entries = slot_ref.shape[-1]
    me = lax.axis_index("gz")
    owners = [owner_ref[0, 0, 0, e] for e in range(entries)]
    for axis in range(2):
        odd = jnp.int32(0)
        for e in range(entries):
            odd = odd | jnp.where(owners[e] >= 0, start_ref[axis, 0, e] & 1, 0)
        parity[axis] = odd
    for distance in range(ring):
        target = lax.rem(me + distance, ring)
        found = jnp.int32(0)
        for e in range(entries):
            picks[found] = e
            found = found + (owners[e] == target).astype(jnp.int32)
        for c in range(capacity):
            held = c < found
            e = jnp.where(held, picks[c], 0)
            lists[distance][4 * c] = jnp.maximum(slot_ref[0, 0, 0, e], 0)
            for axis in range(3):
                lists[distance][4 * c + 1 + axis] = jnp.where(held, start_ref[axis, 0, e], FAR)


def project_kernel(ring, capacity, columns, *refs):
    lists, thermal, outs, both = refs[:ring], refs[ring], refs[ring + 1 : -1], refs[-1]
    tall = 2 * ROWS
    shape = (2 * tall, LANES)
    row = lax.broadcasted_iota(jnp.int32, shape, 0)
    node_x = ((row & 1) << 3) + (lax.broadcasted_iota(jnp.int32, shape, 1) >> log2(NODES))
    plane = lax.broadcasted_iota(jnp.int32, (tall, LANES), 0) >> 1
    cell_y = lax.broadcasted_iota(jnp.int32, (NODES, LANES), 1)
    node_y = 2 * lax.broadcasted_iota(jnp.int32, (NODES, LANES), 0)
    for distance in range(ring):
        total = None
        for c in range(capacity):
            slot, z, x, y = (lists[distance][4 * c + i] for i in range(4))
            rise = half_up(z)
            planes = pltpu.roll(thermal[slot], (2 * rise) & (2 * NODES - 1), 0)[:tall]
            planes = jnp.where((plane >= rise) & (plane < rise + NODES), planes, 0.0)
            coarse = planes.astype(jnp.bfloat16).astype(jnp.float32)
            pair = jnp.concatenate([coarse, planes - coarse], axis=0).astype(jnp.bfloat16)
            shift = half_up(x)
            spread = jnp.concatenate(
                [pair * (node_x == j - shift).astype(jnp.float32).astype(jnp.bfloat16) for j in range(columns)],
                axis=0,
            )
            distance_y = (cell_y - y - node_y).astype(jnp.float32)
            hat = jnp.maximum(0.0, 1.0 - 0.5 * jnp.abs(distance_y)).astype(jnp.bfloat16)
            weight = jnp.concatenate([hat] * (LANES // NODES), axis=0)
            part = jnp.dot(spread, weight, preferred_element_type=jnp.float32)
            total = part if total is None else total + part
        total = total.reshape(columns, 2, tall, LANES)
        both[distance] = (total[:, 0] + total[:, 1]).reshape(columns * tall, LANES)
        even, odd = (both[distance, pl.ds(i, columns * ROWS, stride=2), :] for i in range(2))
        outs[distance][...] = (even + odd).reshape(columns, ROWS, LANES)


def is_odd(axis):
    return (lax.axis_index(axis) & 1) == 1


class Faces:
    def __init__(self, count, layers, breadth, x_low, x_high, y_out, z_first, z_second):
        self.count, self.layers, self.breadth = count, layers, breadth
        self.halves = breadth // ROWS
        self.width = 2 * layers * self.halves
        self.per = LANES // self.width
        self.groups = -(-count // self.per)
        self.x_low, self.x_high, self.y_out = x_low, x_high, y_out
        self.z_first, self.z_second = z_first, z_second

    def lane(self, f, z, half):
        return (f % self.per) * self.width + 2 * (z * self.halves + half)

    def pack(self, fields, extra):
        lanes = lax.broadcasted_iota(jnp.int32, (ROWS, LANES), 1)
        odd = is_odd("gz")
        packed = [None] * self.groups
        for f in range(self.count):
            source = fields.at[f] if f < self.count - 1 else extra
            flat = source.reshape(self.layers * self.breadth, LANES)
            self.x_low[f] = flat[pl.ds(0, self.layers, stride=self.breadth), :]
            self.x_high[f] = flat[pl.ds(self.breadth - 1, self.layers, stride=self.breadth), :]
            low, high = source[0], source[self.layers - 1]
            self.z_first[f] = jnp.where(odd, low, high)
            self.z_second[f] = jnp.where(odd, high, low)
            group = f // self.per
            for z in range(self.layers):
                for half in range(self.halves):
                    k = self.lane(f, z, half)
                    turned = pltpu.roll(source[z, half * ROWS : (half + 1) * ROWS, :], k + 1, 1)
                    known = packed[group]
                    packed[group] = turned if known is None else jnp.where(lanes >> 1 == k >> 1, turned, known)
        for group in range(self.groups):
            self.y_out[group] = packed[group]


def split_x(refs, together):
    if together:
        return (refs[0].at[0], refs[0].at[1]), refs[1:]
    return (refs[0], refs[1]), refs[2:]


def pack_kernel(together, grains, solute, mixed, *rest):
    (x_low, x_high), (y_out, z_first, z_second) = split_x(rest, together)
    orders, layers, breadth, _ = grains.shape
    for z in range(layers):
        squares = None
        for f in range(orders):
            cells = grains[f, z]
            squares = cells * cells if squares is None else squares + cells * cells
        mixed[z] = solute[z] - 0.5 * squares
    Faces(orders + 1, layers, breadth, x_low, x_high, y_out, z_first, z_second).pack(grains, mixed)


def step_kernel(opening, last, together, ring, columns, *refs):
    refs = list(refs)
    take = lambda n: [refs.pop(0) for _ in range(n)]
    fields, solute, mixed = take(3)
    if opening:
        parts = take(ring)
        (parity,) = take(1)
    else:
        (heat,) = take(1)
    if together:
        (arrived,) = take(1)
        x_low, x_high = arrived.at[1], arrived.at[0]
    else:
        x_low, x_high = take(2)
    y_first, y_second, z_first, z_second = take(4)
    fields_out, solute_out = take(2)
    if opening:
        (heat,) = take(1)
    if last:
        (heat_out,) = take(1)
        heat_out[...] = heat[...]
    orders, layers, breadth, _ = fields.shape
    count = orders + 1
    if last:
        wide, turned = take(2)
        faces = Faces(count, layers, breadth, None, None, None, None, None)
    else:
        (mixed_out,) = take(1)
        (out_low, out_high), refs = split_x(refs, together)
        out_y, out_z_first, out_z_second, wide, turned = refs
        faces = Faces(count, layers, breadth, out_low, out_high, out_y, out_z_first, out_z_second)
    lanes = lax.broadcasted_iota(jnp.int32, (ROWS, LANES), 1)

    odd_z, odd_y = is_odd("gz"), is_odd("gy")
    for f in range(count):
        source = fields.at[f] if f < orders else mixed
        wide[f, 1 : layers + 1, ROWS : ROWS + breadth, :] = source[...]
        wide[f, 0, ROWS : ROWS + breadth, :] = jnp.where(odd_z, z_first[f], z_second[f])
        wide[f, layers + 1, ROWS : ROWS + breadth, :] = jnp.where(odd_z, z_second[f], z_first[f])
        wide[f, 1 : layers + 1, ROWS - 1, :] = x_low[f]
        wide[f, 1 : layers + 1, ROWS + breadth, :] = x_high[f]
    for group in range(faces.groups):
        first, second = y_first[group], y_second[group]
        below, above = jnp.where(odd_y, first, second), jnp.where(odd_y, second, first)
        turned[group] = jnp.where((lanes & 1) == 1, pltpu.roll(below, 1, 1), pltpu.roll(above, LANES - 1, 1))

    if opening:
        lattice = parts[0][...]
        for part in parts[1:]:
            lattice = lattice + part[...]
        coarse = lattice.astype(jnp.bfloat16).astype(jnp.float32)
        pair = jnp.concatenate([coarse, lattice - coarse], axis=1)
        pair = pair.reshape(columns * 2 * ROWS, LANES).astype(jnp.bfloat16)
        shape = (layers * breadth, columns * 2 * ROWS)
        cell = lax.broadcasted_iota(jnp.int32, shape, 0)
        node = lax.broadcasted_iota(jnp.int32, shape, 1)

        def hat(position, index, odd):
            gap = (position + odd - 2 * index).astype(jnp.float32)
            return jnp.maximum(0.0, 1.0 - 0.5 * jnp.abs(gap))

        weight = hat(cell >> log2(breadth), node & (ROWS - 1), parity[0]) * hat(
            cell & (breadth - 1), node >> log2(2 * ROWS), parity[1]
        )
        warm = jnp.dot(weight.astype(jnp.bfloat16), pair, preferred_element_type=jnp.float32)
        heat[...] = warm.reshape(layers, breadth, LANES)

    def around(f, z, cells):
        span = slice(ROWS, ROWS + breadth)
        total = wide[f, z, span, :] + wide[f, z + 2, span, :]
        total = total + wide[f, z + 1, ROWS - 1 : ROWS - 1 + breadth, :]
        total = total + wide[f, z + 1, ROWS + 1 : ROWS + 1 + breadth, :]
        sides = []
        for half in range(faces.halves):
            piece = cells[half * ROWS : (half + 1) * ROWS]
            k = faces.lane(f, z, half)
            beyond = pltpu.roll(turned[f // faces.per], LANES - 1 - k, 1)
            below = jnp.where(lanes == 0, beyond, pltpu.roll(piece, 1, 1))
            above = jnp.where(lanes == LANES - 1, beyond, pltpu.roll(piece, LANES - 1, 1))
            sides.append(below + above)
        return total + jnp.concatenate(sides, axis=0)

    def layer(z):
        squares = None
        for f in range(orders):
            cells = fields[f, z]
            squares = cells * cells if squares is None else squares + cells * cells
        here = solute[z]
        pull = 0.04 - 0.1 * squares
        drive = 6.0 * (1.0 - heat[z] - 0.5 * here)
        level = mixed[z]
        fresh = here + 0.15 * (around(orders, z, level) - 6.0 * level)
        solute_out[z] = fresh
        squares = None
        for f in range(orders):
            cells = fields[f, z]
            well = cells * (1.0 - cells)
            value = (
                0.16 * around(f, z, cells)
                + cells * (pull + 0.1 * (cells * cells))
                + well * (drive * well + (0.4 * cells - 0.2))
            )
            fields_out[f, z] = value
            if not last:
                squares = value * value if squares is None else squares + value * value
        if not last:
            mixed_out[z] = fresh - 0.5 * squares

    for z in range(layers):
        layer(z)
    if not last:
        faces.pack(fields_out, mixed_out)


def shape_of(*dims, dtype=jnp.float32):
    return jax.ShapeDtypeStruct(dims, dtype)


def cost(flops, moved):
    return pl.CostEstimate(flops=flops, bytes_accessed=moved, transcendentals=0)


def around_ring(axis, distance):
    count = lax.axis_size(axis)
    return [(i, (i + distance) % count) for i in range(count)]


def send(value, axis, pairs):
    return lax.ppermute(value, axis, pairs)


def swaps(axis, closed):
    count = lax.axis_size(axis)
    assert count % 2 == 0
    first = [(i, i ^ 1) for i in range(count)]
    second = [(i, (i + 1 if i % 2 else i - 1) % count) for i in range(count)]
    if not closed:
        second = [(0, 0)] + second[1:-1] + [(count - 1, count - 1)]
    return first, second


def body(grains, solute, thermal, block_slot, block_owner, block_offset):
    ring = lax.axis_size("gz")
    across = lax.axis_size("gx")
    together = across == 2
    orders, layers, breadth, length = grains.shape
    slots = thermal.shape[3]
    capacity = slots // ring
    columns = breadth // 2 + 1
    count = orders + 1
    entries = block_slot.shape[-1]
    assert length == LANES and breadth % ROWS == 0 and layers // 2 + 1 <= ROWS

    routed = pl.pallas_call(
        functools.partial(route_kernel, ring, capacity),
        out_shape=[shape_of(4 * capacity, dtype=jnp.int32)] * ring + [shape_of(2, dtype=jnp.int32)],
        in_specs=[HBM] * 3,
        out_specs=[SMEM] * (ring + 1),
        scratch_shapes=[
            pltpu.SMEM((entries + 1,), jnp.int32),
            pltpu.SMEM(block_slot.shape, jnp.int32),
            pltpu.SMEM(block_owner.shape, jnp.int32),
            pltpu.SMEM((3, 1, entries), jnp.int32),
            pltpu.SemaphoreType.DMA((3,)),
        ],
        name="route",
    )(block_slot, block_owner, block_offset.reshape(3, 1, entries))
    asked, parity = routed[:ring], routed[ring]
    asked = [asked[0]] + [send(asked[d], "gz", around_ring("gz", d)) for d in range(1, ring)]

    sizes = Faces(count, layers, breadth, None, None, None, None, None)
    face_x = [shape_of(2, count, layers, length)] if together else [shape_of(count, layers, length)] * 2
    face_shapes = face_x + [shape_of(sizes.groups, ROWS, LANES)] + [shape_of(count, breadth, length)] * 2
    tile = shape_of(layers, breadth, length)

    packed = pl.pallas_call(
        functools.partial(pack_kernel, together),
        out_shape=[tile] + face_shapes,
        in_specs=[VMEM] * 2,
        out_specs=[VMEM] * (1 + len(face_shapes)),
        cost_estimate=cost(4_000_000, 2_000_000),
        compiler_params=PARAMS,
        name="pack",
    )(grains, solute)

    def exchange(faces):
        y_out, z_first, z_second = faces[-3:]
        y_swaps, z_swaps = swaps("gy", True), swaps("gz", False)
        if together:
            moved = [send(faces[0], "gx", around_ring("gx", 1))]
        else:
            moved = [send(faces[1], "gx", around_ring("gx", 1)), send(faces[0], "gx", around_ring("gx", -1))]
        return moved + [
            send(y_out, "gy", y_swaps[0]),
            send(y_out, "gy", y_swaps[1]),
            send(z_first, "gz", z_swaps[0]),
            send(z_second, "gz", z_swaps[1]),
        ]

    mixed, faces = packed[0], packed[1:]
    arrived = exchange(faces)

    nodes = thermal.reshape(slots, NODES**3 // LANES, LANES)
    assert NODES**2 == 2 * LANES
    lattice = shape_of(columns, ROWS, length)
    parts = pl.pallas_call(
        functools.partial(project_kernel, ring, capacity, columns),
        out_shape=[lattice] * ring,
        in_specs=[SMEM] * ring + [VMEM],
        out_specs=[VMEM] * ring,
        scratch_shapes=[pltpu.VMEM((ring, columns * 2 * ROWS, LANES), jnp.float32)],
        cost_estimate=cost(4_000_000, 1_000_000),
        compiler_params=PARAMS,
        name="project",
    )(*asked, nodes)
    parts = [parts[0]] + [send(parts[d], "gz", around_ring("gz", -d)) for d in range(1, ring)]

    fields, heat = grains, None
    for repeat in range(STEPS):
        first, last = repeat == 0, repeat == STEPS - 1
        extra = list(parts) + [parity] if first else [heat]
        extra_specs = [VMEM] * ring + [SMEM] if first else [VMEM]
        out_shape = [shape_of(*grains.shape), tile]
        if first or last:
            out_shape = out_shape + [tile]
        if not last:
            out_shape = out_shape + [tile] + face_shapes
        outs = pl.pallas_call(
            functools.partial(step_kernel, first, last, together, ring, columns),
            out_shape=out_shape,
            in_specs=[VMEM] * 3 + extra_specs + [VMEM] * len(arrived),
            out_specs=[VMEM] * len(out_shape),
            scratch_shapes=[
                pltpu.VMEM((count, layers + 2, breadth + 2 * ROWS, LANES), jnp.float32),
                pltpu.VMEM((sizes.groups, ROWS, LANES), jnp.float32),
            ],
            cost_estimate=cost(8_000_000, 3_000_000),
            compiler_params=PARAMS,
        )(fields, solute, mixed, *extra, *arrived)
        fields, solute = outs[:2]
        outs = list(outs[2:])
        if first or last:
            heat = outs.pop(0)
        if not last:
            mixed, faces = outs[0], outs[1:]
            arrived = exchange(faces)
    return (fields, solute, heat)


def solution(mesh):
    in_specs = (
        P(None, "gz", "gx", "gy"),
        P("gz", "gx", "gy"),
        P("gz", "gx", "gy", None, None),
        P("gz", "gx", "gy", None),
        P("gz", "gx", "gy", None),
        P("gz", "gx", "gy", None, None),
    )
    out_specs = (P(None, "gz", "gx", "gy"), P("gz", "gx", "gy"), P("gz", "gx", "gy"))

    return jax.shard_map(body, mesh=mesh, in_specs=in_specs, out_specs=out_specs, check_vma=False)
```

profile of v0, /device:TPU:0, one launch (start us, length us, event | category | flops | bytes accessed | tf_op | source)
XLA Modules:
  0.0 57.0 jit_solution(17540237512480538933)
XLA Ops:
  0.6 1.1 %copy-done = f32[12,8,16,128]{3,2,1,0:T(8,128)S(1)} copy-done((f32[12,8,16,128]{3,2,1,0:T(8,128)S(1)}, f32[12,8,16,128]{3,2,1,0:T(8,128)}, u32[]{:S(2)}) %copy-start) | copy-done | bytes 786456
  1.8 0.8 %copy-done.3 = f32[8,16,128]{2,1,0:T(8,128)S(1)} copy-done((f32[8,16,128]{2,1,0:T(8,128)S(1)}, f32[8,16,128]{2,1,0:T(8,128)}, u32[]{:S(2)}) %copy-start.3) | copy-done | bytes 65560
  2.6 0.3 pack.1
  2.9 3.0 %collective-permute-start.6 = (f32[2,13,8,128]{3,2,1,0:T(8,128)S(1)}, f32[2,13,8,128]{3,2,1,0:T(8,128)S(1)}, u32[]{:S(2)}, u32[]{:S(2)}) collective-permute-start(f32[2,13,8,128]{3,2,1,0:T(8,128)S(1)} %get-tuple-element.42), channel_id=1, source_target_pairs={{0,16},{16,0},{1,17},{17,1},{2,18},{18,2},{3,19},{19,3},{4,20},{20... | collective-permute-start | bytes 319496 | tf_op jit(solution)/shard_map/ppermute | solution.py:286
  5.9 1.6 %collective-permute-start.9 = (f32[13,16,128]{2,1,0:T(8,128)S(1)}, f32[13,16,128]{2,1,0:T(8,128)S(1)}, u32[]{:S(2)}, u32[]{:S(2)}) collective-permute-start(f32[13,16,128]{2,1,0:T(8,128)S(1)} %get-tuple-element.44), channel_id=1, source_target_pairs={{0,1},{1,0},{2,3},{3,2},{4,5},{5,4},{6,7},{7,6},{8,9},{9,8},{10,11... | collective-permute-start | bytes 319496 | tf_op jit(solution)/shard_map/ppermute | solution.py:286
  7.5 0.7 %collective-permute-start.10 = (f32[13,16,128]{2,1,0:T(8,128)S(1)}, f32[13,16,128]{2,1,0:T(8,128)S(1)}, u32[]{:S(2)}, u32[]{:S(2)}) collective-permute-start(f32[13,16,128]{2,1,0:T(8,128)S(1)} %get-tuple-element.45), channel_id=1, source_target_pairs={{0,0},{1,2},{2,1},{3,3},{4,4},{5,6},{6,5},{7,7},{8,8},{9,10},{10,9... | collective-permute-start | bytes 319496 | tf_op jit(solution)/shard_map/ppermute | solution.py:286
  8.2 1.6 %route.1 = (s32[20]{0:T(128)}, s32[20]{0:T(128)}, s32[20]{0:T(128)}, s32[20]{0:T(128)}, s32[2]{0:T(128)}) custom-call(s32[1,1,1,20]{3,2,1,0:T(1,128)} %refs_0_.2, s32[1,1,1,20]{3,2,1,0:T(1,128)} %refs_1_.2, s32[3,1,20]{2,1,0:T(1,128)} %bitcast.3), custom_call_target="tpu_custom_call" | custom-call | tf_op jit(solution)/shard_map/route/pallas_call | solution.py:311
  9.8 0.0 copy-start.9
  9.8 0.6 %copy-done.9 = s32[20]{0:T(128)S(1)} copy-done((s32[20]{0:T(128)S(1)}, s32[20]{0:T(128)}, u32[]{:S(2)}) %copy-start.9) | copy-done | bytes 104
  10.5 4.4 %collective-permute-start = (s32[20]{0:T(128)S(1)}, s32[20]{0:T(128)S(1)}, u32[]{:S(2)}, u32[]{:S(2)}) collective-permute-start(s32[20]{0:T(128)S(1)} %copy-done.9), channel_id=1, source_target_pairs={{0,1},{1,2},{2,3},{3,0},{4,5},{5,6},{6,7},{7,4},{8,9},{9,10},{10,1... | collective-permute-start | bytes 248 | tf_op jit(solution)/shard_map/ppermute | solution.py:286
  14.9 0.1 collective-permute-start.1
  15.0 1.2 %collective-permute-done.refs_1_ = s32[20]{0:T(128)S(1)} collective-permute-done((s32[20]{0:T(128)S(1)}, s32[20]{0:T(128)S(1)}, u32[]{:S(2)}, u32[]{:S(2)}) %collective-permute-start) | collective-permute-done | bytes 112 | tf_op jit(solution)/shard_map/ppermute | solution.py:286
  16.2 1.7 %collective-permute-start.2 = (s32[20]{0:T(128)S(1)}, s32[20]{0:T(128)S(1)}, u32[]{:S(2)}, u32[]{:S(2)}) collective-permute-start(s32[20]{0:T(128)S(1)} %copy-done.7), channel_id=1, source_target_pairs={{0,3},{1,0},{2,1},{3,2},{4,7},{5,4},{6,5},{7,6},{8,11},{9,8},{10,9... | collective-permute-start | bytes 248 | tf_op jit(solution)/shard_map/ppermute | solution.py:286
  17.9 1.4 %collective-permute-done.1.refs_2_ = s32[20]{0:T(128)S(1)} collective-permute-done((s32[20]{0:T(128)S(1)}, s32[20]{0:T(128)S(1)}, u32[]{:S(2)}, u32[]{:S(2)}) %collective-permute-start.1) | collective-permute-done | bytes 112 | tf_op jit(solution)/shard_map/ppermute | solution.py:286
  19.3 0.6 %collective-permute-done.2.refs_3_ = s32[20]{0:T(128)S(1)} collective-permute-done((s32[20]{0:T(128)S(1)}, s32[20]{0:T(128)S(1)}, u32[]{:S(2)}, u32[]{:S(2)}) %collective-permute-start.2) | collective-permute-done | bytes 112 | tf_op jit(solution)/shard_map/ppermute | solution.py:286
  20.0 0.7 %copy-done.6 = s32[20]{0:T(128)S(1)} copy-done((s32[20]{0:T(128)S(1)}, s32[20]{0:T(128)}, u32[]{:S(2)}) %copy-start.6) | copy-done | bytes 104
  20.6 1.0 %copy-done.2 = f32[1,1,1,20,4096]{4,2,3,1,0:T(1,128)S(1)} copy-done((f32[1,1,1,20,4096]{4,2,3,1,0:T(1,128)S(1)}, f32[1,1,1,20,4096]{4,2,3,1,0:T(1,128)}, u32[]{:S(2)}) %copy-start.2) | copy-done | bytes 327704
  21.6 1.2 %project.1 = (f32[9,8,128]{2,1,0:T(8,128)S(1)}, f32[9,8,128]{2,1,0:T(8,128)S(1)}, f32[9,8,128]{2,1,0:T(8,128)S(1)}, f32[9,8,128]{2,1,0:T(8,128)S(1)}) custom-call(s32[20]{0:T(128)S(1)} %copy-done.6, s32[20]{0:T(128)S(1)} %collective-permute-done.refs_1_, s32[20]{0:T(128)S(1)} %collective-permute-done.1.refs_2_, s32[20]{0:T(128)S(1)} %collective-permute-done.2.refs_3_, ...), custom_call_target="tpu_custom_call" | custom-call | flops 4000000 | bytes 1000000 | tf_op jit(solution)/shard_map/project/pallas_call | solution.py:363
  22.8 3.3 %collective-permute-start.3 = (f32[9,8,128]{2,1,0:T(8,128)S(1)}, f32[9,8,128]{2,1,0:T(8,128)S(1)}, u32[]{:S(2)}, u32[]{:S(2)}) collective-permute-start(f32[9,8,128]{2,1,0:T(8,128)S(1)} %get-tuple-element.38), channel_id=1, source_target_pairs={{0,3},{1,0},{2,1},{3,2},{4,7},{5,4},{6,5},{7,6},{8,11},{9,8},{10,9... | collective-permute-start | bytes 110600 | tf_op jit(solution)/shard_map/ppermute | solution.py:286
  26.1 0.0 collective-permute-start.8
  26.2 3.3 %collective-permute-done.8.refs_10_ = f32[4,8,128]{2,1,0:T(8,128)S(1)} collective-permute-done((f32[4,8,128]{2,1,0:T(8,128)S(1)}, f32[4,8,128]{2,1,0:T(8,128)S(1)}, u32[]{:S(2)}, u32[]{:S(2)}) %collective-permute-start.8) | collective-permute-done | bytes 16416 | tf_op jit(solution)/shard_map/ppermute | solution.py:286
  29.4 0.1 collective-permute-start.7
  29.5 1.1 %collective-permute-done.7.refs_9_ = f32[4,8,128]{2,1,0:T(8,128)S(1)} collective-permute-done((f32[4,8,128]{2,1,0:T(8,128)S(1)}, f32[4,8,128]{2,1,0:T(8,128)S(1)}, u32[]{:S(2)}, u32[]{:S(2)}) %collective-permute-start.7) | collective-permute-done | bytes 16416 | tf_op jit(solution)/shard_map/ppermute | solution.py:286
  30.6 0.2 collective-permute-start.4
  30.8 0.0 collective-permute-done.3.refs_4_
  30.8 0.4 collective-permute-start.5
  31.2 4.6 %collective-permute-done.4.refs_5_ = f32[9,8,128]{2,1,0:T(8,128)S(1)} collective-permute-done((f32[9,8,128]{2,1,0:T(8,128)S(1)}, f32[9,8,128]{2,1,0:T(8,128)S(1)}, u32[]{:S(2)}, u32[]{:S(2)}) %collective-permute-start.4) | collective-permute-done | bytes 36896 | tf_op jit(solution)/shard_map/ppermute | solution.py:286
  35.8 0.7 %collective-permute-done.5.refs_6_ = f32[9,8,128]{2,1,0:T(8,128)S(1)} collective-permute-done((f32[9,8,128]{2,1,0:T(8,128)S(1)}, f32[9,8,128]{2,1,0:T(8,128)S(1)}, u32[]{:S(2)}, u32[]{:S(2)}) %collective-permute-start.5) | collective-permute-done | bytes 36896 | tf_op jit(solution)/shard_map/ppermute | solution.py:286
  36.6 0.0 collective-permute-done.9.refs_11_
  36.6 0.0 collective-permute-done.10.refs_12_
  36.6 0.6 %copy-done.5 = s32[2]{0:T(128)S(1)} copy-done((s32[2]{0:T(128)S(1)}, s32[2]{0:T(128)}, u32[]{:S(2)}) %copy-start.5) | copy-done | bytes 32
  37.3 1.9 %shard_map.85 = (f32[12,8,16,128]{3,2,1,0:T(8,128)S(1)}, f32[8,16,128]{2,1,0:T(8,128)S(1)}, f32[8,16,128]{2,1,0:T(8,128)S(1)}, f32[8,16,128]{2,1,0:T(8,128)S(1)}...) custom-call(f32[12,8,16,128]{3,2,1,0:T(8,128)S(1)} %copy-done.1, ...), custom_call_target="tpu_custom_call" | custom-call | flops 8000000 | bytes 3000000 | tf_op jit(solution)/shard_map/pallas_call | solution.py:385
  39.1 0.6 %collective-permute-start.11 = (f32[2,13,8,128]{3,2,1,0:T(8,128)S(1)}, f32[2,13,8,128]{3,2,1,0:T(8,128)S(1)}, u32[]{:S(2)}, u32[]{:S(2)}) collective-permute-start(f32[2,13,8,128]{3,2,1,0:T(8,128)S(1)} %get-tuple-element.50), channel_id=1, source_target_pairs={{0,16},{16,0},{1,17},{17,1},{2,18},{18,2},{3,19},{19,3},{4,20},{20... | collective-permute-start | bytes 319496 | tf_op jit(solution)/shard_map/ppermute | solution.py:286
  39.7 0.0 collective-permute-start.14
  39.7 0.7 %collective-permute-start.15 = (f32[13,16,128]{2,1,0:T(8,128)S(1)}, f32[13,16,128]{2,1,0:T(8,128)S(1)}, u32[]{:S(2)}, u32[]{:S(2)}) collective-permute-start(f32[13,16,128]{2,1,0:T(8,128)S(1)} %get-tuple-element.53), channel_id=1, source_target_pairs={{0,0},{1,2},{2,1},{3,3},{4,4},{5,6},{6,5},{7,7},{8,8},{9,10},{10,9... | collective-permute-start | bytes 319496 | tf_op jit(solution)/shard_map/ppermute | solution.py:286
  40.4 0.1 collective-permute-start.13
  40.5 1.5 %collective-permute-start.12 = (f32[4,8,128]{2,1,0:T(8,128)S(1)}, f32[4,8,128]{2,1,0:T(8,128)S(1)}, u32[]{:S(2)}, u32[]{:S(2)}) collective-permute-start(f32[4,8,128]{2,1,0:T(8,128)S(1)} %get-tuple-element.51), channel_id=1, source_target_pairs={{0,4},{4,0},{8,12},{12,8},{1,5},{5,1},{9,13},{13,9},{2,6},{6,2},{1... | collective-permute-start | bytes 49160 | tf_op jit(solution)/shard_map/ppermute | solution.py:286
  42.0 1.8 %collective-permute-done.13.refs_6_ = f32[4,8,128]{2,1,0:T(8,128)S(1)} collective-permute-done((f32[4,8,128]{2,1,0:T(8,128)S(1)}, f32[4,8,128]{2,1,0:T(8,128)S(1)}, u32[]{:S(2)}, u32[]{:S(2)}) %collective-permute-start.13) | collective-permute-done | bytes 16416 | tf_op jit(solution)/shard_map/ppermute | solution.py:286
  43.8 0.1 collective-permute-done.11.refs_4_
  43.9 0.5 collective-permute-done.14.refs_7_
  44.4 1.3 %shard_map.86 = (f32[12,8,16,128]{3,2,1,0:T(8,128)S(1)}, f32[8,16,128]{2,1,0:T(8,128)S(1)}, f32[8,16,128]{2,1,0:T(8,128)S(1)}, f32[2,13,8,128]{3,2,1,0:T(8,128)S...) custom-call(f32[12,8,16,128]{3,2,1,0:T(8,128)S(1)} %get-tuple-element.46.refs_0_, ...), custom_call_target="tpu_custom_call" | custom-call | flops 8000000 | bytes 3000000 | tf_op jit(solution)/shard_map/pallas_call | solution.py:385
  45.7 1.6 %collective-permute-start.16 = (f32[2,13,8,128]{3,2,1,0:T(8,128)S(1)}, f32[2,13,8,128]{3,2,1,0:T(8,128)S(1)}, u32[]{:S(2)}, u32[]{:S(2)}) collective-permute-start(f32[2,13,8,128]{3,2,1,0:T(8,128)S(1)} %get-tuple-element.57), channel_id=1, source_target_pairs={{0,16},{16,0},{1,17},{17,1},{2,18},{18,2},{3,19},{19,3},{4,20},{20... | collective-permute-start | bytes 319496 | tf_op jit(solution)/shard_map/ppermute | solution.py:286
  47.3 3.9 %collective-permute-start.19 = (f32[13,16,128]{2,1,0:T(8,128)S(1)}, f32[13,16,128]{2,1,0:T(8,128)S(1)}, u32[]{:S(2)}, u32[]{:S(2)}) collective-permute-start(f32[13,16,128]{2,1,0:T(8,128)S(1)} %get-tuple-element.59), channel_id=1, source_target_pairs={{0,1},{1,0},{2,3},{3,2},{4,5},{5,4},{6,7},{7,6},{8,9},{9,8},{10,11... | collective-permute-start | bytes 319496 | tf_op jit(solution)/shard_map/ppermute | solution.py:286
  51.2 0.7 %collective-permute-start.20 = (f32[13,16,128]{2,1,0:T(8,128)S(1)}, f32[13,16,128]{2,1,0:T(8,128)S(1)}, u32[]{:S(2)}, u32[]{:S(2)}) collective-permute-start(f32[13,16,128]{2,1,0:T(8,128)S(1)} %get-tuple-element.60), channel_id=1, source_target_pairs={{0,0},{1,2},{2,1},{3,3},{4,4},{5,6},{6,5},{7,7},{8,8},{9,10},{10,9... | collective-permute-start | bytes 319496 | tf_op jit(solution)/shard_map/ppermute | solution.py:286
  51.8 0.1 collective-permute-start.18
  51.9 1.5 %collective-permute-start.17 = (f32[4,8,128]{2,1,0:T(8,128)S(1)}, f32[4,8,128]{2,1,0:T(8,128)S(1)}, u32[]{:S(2)}, u32[]{:S(2)}) collective-permute-start(f32[4,8,128]{2,1,0:T(8,128)S(1)} %get-tuple-element.58), channel_id=1, source_target_pairs={{0,4},{4,0},{8,12},{12,8},{1,5},{5,1},{9,13},{13,9},{2,6},{6,2},{1... | collective-permute-start | bytes 49160 | tf_op jit(solution)/shard_map/ppermute | solution.py:286
  53.4 1.8 %collective-permute-done.18.refs_6_ = f32[4,8,128]{2,1,0:T(8,128)S(1)} collective-permute-done((f32[4,8,128]{2,1,0:T(8,128)S(1)}, f32[4,8,128]{2,1,0:T(8,128)S(1)}, u32[]{:S(2)}, u32[]{:S(2)}) %collective-permute-start.18) | collective-permute-done | bytes 16416 | tf_op jit(solution)/shard_map/ppermute | solution.py:286
  55.2 1.7 %shard_map.87 = (f32[12,8,16,128]{3,2,1,0:T(8,128)}, f32[8,16,128]{2,1,0:T(8,128)}, f32[8,16,128]{2,1,0:T(8,128)}) custom-call(f32[12,8,16,128]{3,2,1,0:T(8,128)S(1)} %get-tuple-element.54.refs_0_, f32[8,16,128]{2,1,0:T(8,128)S(1)} %get-tuple-element.55.refs_1_, f32[8,16,128]{2,1,0:T(8,128)S(1)} %get-tuple-element.56.refs_2_, ...), custom_call_target="tpu_custom_call" | custom-call | flops 8000000 | bytes 3000000 | tf_op jit(solution)/shard_map/pallas_call | solution.py:385
  (20 shorter events, 0.0 us)
Async XLA Ops:
  0.6 1.1 %copy-start = (f32[12,8,16,128]{3,2,1,0:T(8,128)S(1)}, f32[12,8,16,128]{3,2,1,0:T(8,128)}, u32[]{:S(2)}) copy-start(f32[12,8,16,128]{3,2,1,0:T(8,128)} %refs_0_.3) | copy-start | bytes 2359300
  1.8 0.8 %copy-start.3 = (f32[8,16,128]{2,1,0:T(8,128)S(1)}, f32[8,16,128]{2,1,0:T(8,128)}, u32[]{:S(2)}) copy-start(f32[8,16,128]{2,1,0:T(8,128)} %refs_1_.3) | copy-start | bytes 196612
  2.6 34.0 %copy-start.1 = (f32[12,8,16,128]{3,2,1,0:T(8,128)S(1)}, f32[12,8,16,128]{3,2,1,0:T(8,128)}, u32[]{:S(2)}) copy-start(f32[12,8,16,128]{3,2,1,0:T(8,128)} %refs_0_.3) | copy-start | bytes 2359300
  2.9 33.7 %collective-permute-start.6 = (f32[2,13,8,128]{3,2,1,0:T(8,128)S(1)}, f32[2,13,8,128]{3,2,1,0:T(8,128)S(1)}, u32[]{:S(2)}, u32[]{:S(2)}) collective-permute-start(f32[2,13,8,128]{3,2,1,0:T(8,128)S(1)} %get-tuple-element.42), channel_id=1, source_target_pairs={{0,16},{16,0},{1,17},{17,1},{2,18},{18,2},{3,19},{19,3},{4,20},{20... | collective-permute-start | bytes 319496 | tf_op jit(solution)/shard_map/ppermute | solution.py:286
  5.9 30.6 %collective-permute-start.9 = (f32[13,16,128]{2,1,0:T(8,128)S(1)}, f32[13,16,128]{2,1,0:T(8,128)S(1)}, u32[]{:S(2)}, u32[]{:S(2)}) collective-permute-start(f32[13,16,128]{2,1,0:T(8,128)S(1)} %get-tuple-element.44), channel_id=1, source_target_pairs={{0,1},{1,0},{2,3},{3,2},{4,5},{5,4},{6,7},{7,6},{8,9},{9,8},{10,11... | collective-permute-start | bytes 319496 | tf_op jit(solution)/shard_map/ppermute | solution.py:286
  7.5 29.1 %collective-permute-start.10 = (f32[13,16,128]{2,1,0:T(8,128)S(1)}, f32[13,16,128]{2,1,0:T(8,128)S(1)}, u32[]{:S(2)}, u32[]{:S(2)}) collective-permute-start(f32[13,16,128]{2,1,0:T(8,128)S(1)} %get-tuple-element.45), channel_id=1, source_target_pairs={{0,0},{1,2},{2,1},{3,3},{4,4},{5,6},{6,5},{7,7},{8,8},{9,10},{10,9... | collective-permute-start | bytes 319496 | tf_op jit(solution)/shard_map/ppermute | solution.py:286
  9.8 0.7 %copy-start.9 = (s32[20]{0:T(128)S(1)}, s32[20]{0:T(128)}, u32[]{:S(2)}) copy-start(s32[20]{0:T(128)} %get-tuple-element.34) | copy-start | bytes 244
  10.5 4.4 %copy-start.8 = (s32[20]{0:T(128)S(1)}, s32[20]{0:T(128)}, u32[]{:S(2)}) copy-start(s32[20]{0:T(128)} %get-tuple-element.35) | copy-start | bytes 244
  10.5 5.7 %collective-permute-start = (s32[20]{0:T(128)S(1)}, s32[20]{0:T(128)S(1)}, u32[]{:S(2)}, u32[]{:S(2)}) collective-permute-start(s32[20]{0:T(128)S(1)} %copy-done.9), channel_id=1, source_target_pairs={{0,1},{1,2},{2,3},{3,0},{4,5},{5,6},{6,7},{7,4},{8,9},{9,10},{10,1... | collective-permute-start | bytes 248 | tf_op jit(solution)/shard_map/ppermute | solution.py:286
  14.9 1.3 %copy-start.7 = (s32[20]{0:T(128)S(1)}, s32[20]{0:T(128)}, u32[]{:S(2)}) copy-start(s32[20]{0:T(128)} %get-tuple-element.36) | copy-start | bytes 244
  14.9 4.5 %collective-permute-start.1 = (s32[20]{0:T(128)S(1)}, s32[20]{0:T(128)S(1)}, u32[]{:S(2)}, u32[]{:S(2)}) collective-permute-start(s32[20]{0:T(128)S(1)} %copy-done.8), channel_id=1, source_target_pairs={{0,2},{1,3},{2,0},{3,1},{4,6},{5,7},{6,4},{7,5},{8,10},{9,11},{10,... | collective-permute-start | bytes 248 | tf_op jit(solution)/shard_map/ppermute | solution.py:286
  16.2 3.8 %collective-permute-start.2 = (s32[20]{0:T(128)S(1)}, s32[20]{0:T(128)S(1)}, u32[]{:S(2)}, u32[]{:S(2)}) collective-permute-start(s32[20]{0:T(128)S(1)} %copy-done.7), channel_id=1, source_target_pairs={{0,3},{1,0},{2,1},{3,2},{4,7},{5,4},{6,5},{7,6},{8,11},{9,8},{10,9... | collective-permute-start | bytes 248 | tf_op jit(solution)/shard_map/ppermute | solution.py:286
  20.0 0.7 %copy-start.6 = (s32[20]{0:T(128)S(1)}, s32[20]{0:T(128)}, u32[]{:S(2)}) copy-start(s32[20]{0:T(128)} %get-tuple-element.33.refs_0_) | copy-start | bytes 244
  20.6 1.0 %copy-start.2 = (f32[1,1,1,20,4096]{4,2,3,1,0:T(1,128)S(1)}, f32[1,1,1,20,4096]{4,2,3,1,0:T(1,128)}, u32[]{:S(2)}) copy-start(f32[1,1,1,20,4096]{4,2,3,1,0:T(1,128)} %param.8) | copy-start | bytes 983044
  21.6 15.0 %copy-start.4 = (f32[8,16,128]{2,1,0:T(8,128)S(1)}, f32[8,16,128]{2,1,0:T(8,128)}, u32[]{:S(2)}) copy-start(f32[8,16,128]{2,1,0:T(8,128)} %refs_1_.3) | copy-start | bytes 196612
  22.8 8.0 %collective-permute-start.3 = (f32[9,8,128]{2,1,0:T(8,128)S(1)}, f32[9,8,128]{2,1,0:T(8,128)S(1)}, u32[]{:S(2)}, u32[]{:S(2)}) collective-permute-start(f32[9,8,128]{2,1,0:T(8,128)S(1)} %get-tuple-element.38), channel_id=1, source_target_pairs={{0,3},{1,0},{2,1},{3,2},{4,7},{5,4},{6,5},{7,6},{8,11},{9,8},{10,9... | collective-permute-start | bytes 110600 | tf_op jit(solution)/shard_map/ppermute | solution.py:286
  26.1 3.3 %collective-permute-start.8 = (f32[4,8,128]{2,1,0:T(8,128)S(1)}, f32[4,8,128]{2,1,0:T(8,128)S(1)}, u32[]{:S(2)}, u32[]{:S(2)}) collective-permute-start(f32[4,8,128]{2,1,0:T(8,128)S(1)} %get-tuple-element.43), channel_id=1, source_target_pairs={{0,12},{4,8},{8,4},{12,0},{1,13},{5,9},{9,5},{13,1},{2,14},{6,10},... | collective-permute-start | bytes 49160 | tf_op jit(solution)/shard_map/ppermute | solution.py:286
  29.4 1.2 %collective-permute-start.7 = (f32[4,8,128]{2,1,0:T(8,128)S(1)}, f32[4,8,128]{2,1,0:T(8,128)S(1)}, u32[]{:S(2)}, u32[]{:S(2)}) collective-permute-start(f32[4,8,128]{2,1,0:T(8,128)S(1)} %get-tuple-element.43), channel_id=1, source_target_pairs={{0,4},{4,0},{8,12},{12,8},{1,5},{5,1},{9,13},{13,9},{2,6},{6,2},{1... | collective-permute-start | bytes 49160 | tf_op jit(solution)/shard_map/ppermute | solution.py:286
  30.6 5.3 %collective-permute-start.4 = (f32[9,8,128]{2,1,0:T(8,128)S(1)}, f32[9,8,128]{2,1,0:T(8,128)S(1)}, u32[]{:S(2)}, u32[]{:S(2)}) collective-permute-start(f32[9,8,128]{2,1,0:T(8,128)S(1)} %get-tuple-element.39), channel_id=1, source_target_pairs={{0,2},{1,3},{2,0},{3,1},{4,6},{5,7},{6,4},{7,5},{8,10},{9,11},{10,... | collective-permute-start | bytes 110600 | tf_op jit(solution)/shard_map/ppermute | solution.py:286
  30.8 5.8 %collective-permute-start.5 = (f32[9,8,128]{2,1,0:T(8,128)S(1)}, f32[9,8,128]{2,1,0:T(8,128)S(1)}, u32[]{:S(2)}, u32[]{:S(2)}) collective-permute-start(f32[9,8,128]{2,1,0:T(8,128)S(1)} %get-tuple-element.40), channel_id=1, source_target_pairs={{0,1},{1,2},{2,3},{3,0},{4,5},{5,6},{6,7},{7,4},{8,9},{9,10},{10,1... | collective-permute-start | bytes 110600 | tf_op jit(solution)/shard_map/ppermute | solution.py:286
  36.6 0.7 %copy-start.5 = (s32[2]{0:T(128)S(1)}, s32[2]{0:T(128)}, u32[]{:S(2)}) copy-start(s32[2]{0:T(128)} %get-tuple-element.41.refs_7_) | copy-start | bytes 28
  39.1 4.8 %collective-permute-start.11 = (f32[2,13,8,128]{3,2,1,0:T(8,128)S(1)}, f32[2,13,8,128]{3,2,1,0:T(8,128)S(1)}, u32[]{:S(2)}, u32[]{:S(2)}) collective-permute-start(f32[2,13,8,128]{3,2,1,0:T(8,128)S(1)} %get-tuple-element.50), channel_id=1, source_target_pairs={{0,16},{16,0},{1,17},{17,1},{2,18},{18,2},{3,19},{19,3},{4,20},{20... | collective-permute-start | bytes 319496 | tf_op jit(solution)/shard_map/ppermute | solution.py:286
  39.7 4.7 %collective-permute-start.14 = (f32[13,16,128]{2,1,0:T(8,128)S(1)}, f32[13,16,128]{2,1,0:T(8,128)S(1)}, u32[]{:S(2)}, u32[]{:S(2)}) collective-permute-start(f32[13,16,128]{2,1,0:T(8,128)S(1)} %get-tuple-element.52), channel_id=1, source_target_pairs={{0,1},{1,0},{2,3},{3,2},{4,5},{5,4},{6,7},{7,6},{8,9},{9,8},{10,11... | collective-permute-start | bytes 319496 | tf_op jit(solution)/shard_map/ppermute | solution.py:286
  39.7 4.7 %collective-permute-start.15 = (f32[13,16,128]{2,1,0:T(8,128)S(1)}, f32[13,16,128]{2,1,0:T(8,128)S(1)}, u32[]{:S(2)}, u32[]{:S(2)}) collective-permute-start(f32[13,16,128]{2,1,0:T(8,128)S(1)} %get-tuple-element.53), channel_id=1, source_target_pairs={{0,0},{1,2},{2,1},{3,3},{4,4},{5,6},{6,5},{7,7},{8,8},{9,10},{10,9... | collective-permute-start | bytes 319496 | tf_op jit(solution)/shard_map/ppermute | solution.py:286
  40.4 3.4 %collective-permute-start.13 = (f32[4,8,128]{2,1,0:T(8,128)S(1)}, f32[4,8,128]{2,1,0:T(8,128)S(1)}, u32[]{:S(2)}, u32[]{:S(2)}) collective-permute-start(f32[4,8,128]{2,1,0:T(8,128)S(1)} %get-tuple-element.51), channel_id=1, source_target_pairs={{0,12},{4,8},{8,4},{12,0},{1,13},{5,9},{9,5},{13,1},{2,14},{6,10},... | collective-permute-start | bytes 49160 | tf_op jit(solution)/shard_map/ppermute | solution.py:286
  40.5 3.3 %collective-permute-start.12 = (f32[4,8,128]{2,1,0:T(8,128)S(1)}, f32[4,8,128]{2,1,0:T(8,128)S(1)}, u32[]{:S(2)}, u32[]{:S(2)}) collective-permute-start(f32[4,8,128]{2,1,0:T(8,128)S(1)} %get-tuple-element.51), channel_id=1, source_target_pairs={{0,4},{4,0},{8,12},{12,8},{1,5},{5,1},{9,13},{13,9},{2,6},{6,2},{1... | collective-permute-start | bytes 49160 | tf_op jit(solution)/shard_map/ppermute | solution.py:286
  45.7 9.5 %collective-permute-start.16 = (f32[2,13,8,128]{3,2,1,0:T(8,128)S(1)}, f32[2,13,8,128]{3,2,1,0:T(8,128)S(1)}, u32[]{:S(2)}, u32[]{:S(2)}) collective-permute-start(f32[2,13,8,128]{3,2,1,0:T(8,128)S(1)} %get-tuple-element.57), channel_id=1, source_target_pairs={{0,16},{16,0},{1,17},{17,1},{2,18},{18,2},{3,19},{19,3},{4,20},{20... | collective-permute-start | bytes 319496 | tf_op jit(solution)/shard_map/ppermute | solution.py:286
  47.3 8.0 %collective-permute-start.19 = (f32[13,16,128]{2,1,0:T(8,128)S(1)}, f32[13,16,128]{2,1,0:T(8,128)S(1)}, u32[]{:S(2)}, u32[]{:S(2)}) collective-permute-start(f32[13,16,128]{2,1,0:T(8,128)S(1)} %get-tuple-element.59), channel_id=1, source_target_pairs={{0,1},{1,0},{2,3},{3,2},{4,5},{5,4},{6,7},{7,6},{8,9},{9,8},{10,11... | collective-permute-start | bytes 319496 | tf_op jit(solution)/shard_map/ppermute | solution.py:286
  51.2 4.1 %collective-permute-start.20 = (f32[13,16,128]{2,1,0:T(8,128)S(1)}, f32[13,16,128]{2,1,0:T(8,128)S(1)}, u32[]{:S(2)}, u32[]{:S(2)}) collective-permute-start(f32[13,16,128]{2,1,0:T(8,128)S(1)} %get-tuple-element.60), channel_id=1, source_target_pairs={{0,0},{1,2},{2,1},{3,3},{4,4},{5,6},{6,5},{7,7},{8,8},{9,10},{10,9... | collective-permute-start | bytes 319496 | tf_op jit(solution)/shard_map/ppermute | solution.py:286
  51.8 3.4 %collective-permute-start.18 = (f32[4,8,128]{2,1,0:T(8,128)S(1)}, f32[4,8,128]{2,1,0:T(8,128)S(1)}, u32[]{:S(2)}, u32[]{:S(2)}) collective-permute-start(f32[4,8,128]{2,1,0:T(8,128)S(1)} %get-tuple-element.58), channel_id=1, source_target_pairs={{0,12},{4,8},{8,4},{12,0},{1,13},{5,9},{9,5},{13,1},{2,14},{6,10},... | collective-permute-start | bytes 49160 | tf_op jit(solution)/shard_map/ppermute | solution.py:286
  51.9 3.3 %collective-permute-start.17 = (f32[4,8,128]{2,1,0:T(8,128)S(1)}, f32[4,8,128]{2,1,0:T(8,128)S(1)}, u32[]{:S(2)}, u32[]{:S(2)}) collective-permute-start(f32[4,8,128]{2,1,0:T(8,128)S(1)} %get-tuple-element.58), channel_id=1, source_target_pairs={{0,4},{4,0},{8,12},{12,8},{1,5},{5,1},{9,13},{13,9},{2,6},{6,2},{1... | collective-permute-start | bytes 49160 | tf_op jit(solution)/shard_map/ppermute | solution.py:286
where the time goes:
time: 57.3 us; the launch traced here: 57 us
  starting transfers between devices  26.1 us (46%)
  waiting for transfers between devices  17.2 us (30%)
  Pallas kernels  8.02 us (14%)
  local copies, waits for them, and re-layouts  4.89 us (9%)
  between operations  0.77 us (1%)
    ppermute x21, starting transfers between devices, send(): return lax.ppermute(value, axis, pairs)  26.1 us
    ppermute x21, waiting for transfers between devices, send(): return lax.ppermute(value, axis, pairs)  17.2 us
    pallas_call x3, Pallas kernels, body(): pl.pallas_call(functools.partial(step_kernel, first, last, together, ring...  4.89 us
    unnamed x20, local copies, waits for them, and re-layouts  4.89 us
    pallas_call x1, Pallas kernels, body(): pl.pallas_call(functools.partial(route_kernel, ring, capacity), out_shape...  1.61 us
    pallas_call x1, Pallas kernels, body(): pl.pallas_call(functools.partial(project_kernel, ring, capacity, columns)...  1.21 us
  transfers between devices with their start and end apart: 21, of which 11 were waited for; matrix products, arithmetic and copies ran while one was open for 0% of the time, Pallas kernels for 5%

commit v1 on v0

--- a/solution.py
+++ b/solution.py
@@ -30,24 +30,15 @@
     return (start + (start & 1)) >> 1
 
 
-def route_kernel(ring, capacity, *refs):
-    lists, parity, picks = refs[3 : 3 + ring], refs[3 + ring], refs[4 + ring]
-    slot_ref, owner_ref, start_ref, arrivals = refs[5 + ring :]
-    copies = [
-        pltpu.make_async_copy(source, target, arrivals.at[i])
-        for i, (source, target) in enumerate(zip(refs[:3], (slot_ref, owner_ref, start_ref)))
-    ]
-    for copy in copies:
-        copy.start()
-    for copy in copies:
-        copy.wait()
-    entries = slot_ref.shape[-1]
+def route_kernel(ring, capacity, table, *refs):
+    lists, parity, picks = refs[:ring], refs[ring], refs[ring + 1]
+    entries = table.shape[-1]
     me = lax.axis_index("gz")
-    owners = [owner_ref[0, 0, 0, e] for e in range(entries)]
+    owners = [table[1, 0, e] for e in range(entries)]
     for axis in range(2):
         odd = jnp.int32(0)
         for e in range(entries):
-            odd = odd | jnp.where(owners[e] >= 0, start_ref[axis, 0, e] & 1, 0)
+            odd = odd | jnp.where(owners[e] >= 0, table[2 + axis, 0, e] & 1, 0)
         parity[axis] = odd
     for distance in range(ring):
         target = lax.rem(me + distance, ring)
@@ -58,9 +49,9 @@
         for c in range(capacity):
             held = c < found
             e = jnp.where(held, picks[c], 0)
-            lists[distance][4 * c] = jnp.maximum(slot_ref[0, 0, 0, e], 0)
+            lists[distance][4 * c] = jnp.maximum(table[0, 0, e], 0)
             for axis in range(3):
-                lists[distance][4 * c + 1 + axis] = jnp.where(held, start_ref[axis, 0, e], FAR)
+                lists[distance][4 * c + 1 + axis] = jnp.where(held, table[2 + axis, 0, e], FAR)
 
 
 def project_kernel(ring, capacity, columns, *refs):
@@ -175,7 +166,8 @@
         (heat,) = take(1)
     if last:
         (heat_out,) = take(1)
-        heat_out[...] = heat[...]
+        far = fields_out, solute_out
+        leaving, fields_out, solute_out = refs.pop(), refs.pop(), refs.pop()
     orders, layers, breadth, _ = fields.shape
     count = orders + 1
     if last:
@@ -263,9 +255,21 @@
         if not last:
             mixed_out[z] = fresh - 0.5 * squares
 
+    copies = []
+    if last:
+        copies.append(pltpu.make_async_copy(heat, heat_out, leaving.at[layers]))
+        copies[-1].start()
     for z in range(layers):
         layer(z)
-    if not last:
+        if last:
+            copies.append(pltpu.make_async_copy(fields_out.at[:, z], far[0].at[:, z], leaving.at[z]))
+            copies[-1].start()
+    if last:
+        copies.append(pltpu.make_async_copy(solute_out, far[1], leaving.at[layers + 1]))
+        copies[-1].start()
+        for copy in copies:
+            copy.wait()
+    else:
         faces.pack(fields_out, mixed_out)
 
 
@@ -308,20 +312,19 @@
     entries = block_slot.shape[-1]
     assert length == LANES and breadth % ROWS == 0 and layers // 2 + 1 <= ROWS
 
+    table = jnp.concatenate(
+        [array.reshape(-1, 1, entries) for array in (block_slot, block_owner, block_offset)], axis=0
+    )
     routed = pl.pallas_call(
         functools.partial(route_kernel, ring, capacity),
         out_shape=[shape_of(4 * capacity, dtype=jnp.int32)] * ring + [shape_of(2, dtype=jnp.int32)],
-        in_specs=[HBM] * 3,
+        in_specs=[SMEM],
         out_specs=[SMEM] * (ring + 1),
-        scratch_shapes=[
-            pltpu.SMEM((entries + 1,), jnp.int32),
-            pltpu.SMEM(block_slot.shape, jnp.int32),
-            pltpu.SMEM(block_owner.shape, jnp.int32),
-            pltpu.SMEM((3, 1, entries), jnp.int32),
-            pltpu.SemaphoreType.DMA((3,)),
-        ],
+        scratch_shapes=[pltpu.SMEM((entries + 1,), jnp.int32)],
+        compiler_params=PARAMS,
+        cost_estimate=cost(1_000_000_000, 1_000),
         name="route",
-    )(block_slot, block_owner, block_offset.reshape(3, 1, entries))
+    )(table)
     asked, parity = routed[:ring], routed[ring]
     asked = [asked[0]] + [send(asked[d], "gz", around_ring("gz", d)) for d in range(1, ring)]
 
@@ -335,7 +338,7 @@
         out_shape=[tile] + face_shapes,
         in_specs=[VMEM] * 2,
         out_specs=[VMEM] * (1 + len(face_shapes)),
-        cost_estimate=cost(4_000_000, 2_000_000),
+        cost_estimate=cost(400_000_000, 2_000_000),
         compiler_params=PARAMS,
         name="pack",
     )(grains, solute)
@@ -373,6 +376,11 @@
     parts = [parts[0]] + [send(parts[d], "gz", around_ring("gz", -d)) for d in range(1, ring)]
 
     fields, heat = grains, None
+    leaving = [
+        pltpu.VMEM((layers, breadth, length), jnp.float32),
+        pltpu.VMEM(grains.shape, jnp.float32),
+        pltpu.SemaphoreType.DMA((layers + 2,)),
+    ]
     for repeat in range(STEPS):
         first, last = repeat == 0, repeat == STEPS - 1
         extra = list(parts) + [parity] if first else [heat]
@@ -386,11 +394,12 @@
             functools.partial(step_kernel, first, last, together, ring, columns),
             out_shape=out_shape,
             in_specs=[VMEM] * 3 + extra_specs + [VMEM] * len(arrived),
-            out_specs=[VMEM] * len(out_shape),
+            out_specs=[HBM if last else VMEM] * len(out_shape),
             scratch_shapes=[
                 pltpu.VMEM((count, layers + 2, breadth + 2 * ROWS, LANES), jnp.float32),
                 pltpu.VMEM((sizes.groups, ROWS, LANES), jnp.float32),
-            ],
+            ]
+            + leaving * last,
             cost_estimate=cost(8_000_000, 3_000_000),
             compiler_params=PARAMS,
         )(fields, solute, mixed, *extra, *arrived)

time: 57.3 us -> 54.9 us (0.958)
  local copies, waits for them, and re-layouts: 4.89 us -> 2.65 us
  waiting for transfers between devices: 17.2 us -> 18.3 us
  starting transfers between devices: 26.1 us -> 25.1 us
    unnamed x20 -> x16, local copies, waits for them, and re-layouts: 4.89 us -> 2.65 us
    ppermute x21, waiting for transfers between devices: 17.2 us -> 18.3 us  [send(): return lax.ppermute(value, axis, pairs)]
    ppermute x21, starting transfers between devices: 26.1 us -> 25.1 us  [send(): return lax.ppermute(value, axis, pairs)]
where the time goes in v1:
time: 54.9 us; the launch traced here: 54.7 us
  starting transfers between devices  25.1 us (46%)
  waiting for transfers between devices  18.3 us (33%)
  Pallas kernels  7.85 us (14%)
  local copies, waits for them, and re-layouts  2.65 us (5%)
  between operations  0.8 us (1%)
    ppermute x21, starting transfers between devices, send(): return lax.ppermute(value, axis, pairs)  25.1 us
    ppermute x21, waiting for transfers between devices, send(): return lax.ppermute(value, axis, pairs)  18.3 us
    pallas_call x3, Pallas kernels, body(): pl.pallas_call(functools.partial(step_kernel, first, last, together, ring...  4.79 us
    unnamed x16, local copies, waits for them, and re-layouts  2.65 us
    pallas_call x1, Pallas kernels, body(): pl.pallas_call(functools.partial(route_kernel, ring, capacity), out_shape...  1.54 us
    pallas_call x1, Pallas kernels, body(): pl.pallas_call(functools.partial(project_kernel, ring, capacity, columns)...  1.21 us
  transfers between devices with their start and end apart: 21, of which 11 were waited for; matrix products, arithmetic and copies ran while one was open for 0% of the time, Pallas kernels for 5%

profile of v1, /device:TPU:0, one launch (start us, length us, event | category | flops | bytes accessed | tf_op | source)
XLA Modules:
  0.0 54.7 jit_solution(763856974254886655)
XLA Ops:
  0.6 0.0 copy-start
  0.6 1.1 %copy-done = f32[12,8,16,128]{3,2,1,0:T(8,128)S(1)} copy-done((f32[12,8,16,128]{3,2,1,0:T(8,128)S(1)}, f32[12,8,16,128]{3,2,1,0:T(8,128)}, u32[]{:S(2)}) %copy-start) | copy-done | bytes 786456
  1.8 0.8 %copy-done.3 = f32[8,16,128]{2,1,0:T(8,128)S(1)} copy-done((f32[8,16,128]{2,1,0:T(8,128)S(1)}, f32[8,16,128]{2,1,0:T(8,128)}, u32[]{:S(2)}) %copy-start.3) | copy-done | bytes 65560
  2.6 0.3 pack.1
  2.9 3.0 %collective-permute-start.6 = (f32[2,13,8,128]{3,2,1,0:T(8,128)S(1)}, f32[2,13,8,128]{3,2,1,0:T(8,128)S(1)}, u32[]{:S(2)}, u32[]{:S(2)}) collective-permute-start(f32[2,13,8,128]{3,2,1,0:T(8,128)S(1)} %get-tuple-element.42), channel_id=1, source_target_pairs={{0,16},{16,0},{1,17},{17,1},{2,18},{18,2},{3,19},{19,3},{4,20},{20... | collective-permute-start | bytes 319496 | tf_op jit(solution)/shard_map/ppermute | solution.py:290
  5.9 1.6 %collective-permute-start.9 = (f32[13,16,128]{2,1,0:T(8,128)S(1)}, f32[13,16,128]{2,1,0:T(8,128)S(1)}, u32[]{:S(2)}, u32[]{:S(2)}) collective-permute-start(f32[13,16,128]{2,1,0:T(8,128)S(1)} %get-tuple-element.44), channel_id=1, source_target_pairs={{0,1},{1,0},{2,3},{3,2},{4,5},{5,4},{6,7},{7,6},{8,9},{9,8},{10,11... | collective-permute-start | bytes 319496 | tf_op jit(solution)/shard_map/ppermute | solution.py:290
  7.5 0.7 %collective-permute-start.10 = (f32[13,16,128]{2,1,0:T(8,128)S(1)}, f32[13,16,128]{2,1,0:T(8,128)S(1)}, u32[]{:S(2)}, u32[]{:S(2)}) collective-permute-start(f32[13,16,128]{2,1,0:T(8,128)S(1)} %get-tuple-element.45), channel_id=1, source_target_pairs={{0,0},{1,2},{2,1},{3,3},{4,4},{5,6},{6,5},{7,7},{8,8},{9,10},{10,9... | collective-permute-start | bytes 319496 | tf_op jit(solution)/shard_map/ppermute | solution.py:290
  8.2 0.0 copy-start.5
  8.2 0.0 copy-start.6
  8.2 0.0 copy-start.7
  8.2 0.6 %copy-done.5 = s32[1,1,1,3,20]{4,2,3,1,0:T(1,128)S(1)} copy-done((s32[1,1,1,3,20]{4,2,3,1,0:T(1,128)S(1)}, s32[1,1,1,3,20]{4,2,3,1,0:T(1,128)}, u32[]{:S(2)}) %copy-start.5) | copy-done | bytes 264
  8.9 0.0 copy-done.7
  8.9 0.0 copy-start.2
  8.9 0.0 copy-start.1
  8.9 1.5 %route.1 = (s32[20]{0:T(128)S(1)}, s32[20]{0:T(128)S(1)}, s32[20]{0:T(128)S(1)}, s32[20]{0:T(128)S(1)}, s32[2]{0:T(128)S(1)}) custom-call(s32[5,1,20]{2,1,0:T(1,128)S(1)} %pad_add_fusion.table), custom_call_target="tpu_custom_call" | custom-call | flops 1000000000 | bytes 1000 | tf_op jit(solution)/shard_map/route/pallas_call | solution.py:318
  10.5 4.4 %collective-permute-start = (s32[20]{0:T(128)S(1)}, s32[20]{0:T(128)S(1)}, u32[]{:S(2)}, u32[]{:S(2)}) collective-permute-start(s32[20]{0:T(128)S(1)} %get-tuple-element.34), channel_id=1, source_target_pairs={{0,1},{1,2},{2,3},{3,0},{4,5},{5,6},{6,7},{7,4},{8,9},{9,10},{10,1... | collective-permute-start | bytes 248 | tf_op jit(solution)/shard_map/ppermute | solution.py:290
  14.9 0.0 collective-permute-start.1
  14.9 1.3 %collective-permute-done.refs_1_ = s32[20]{0:T(128)S(1)} collective-permute-done((s32[20]{0:T(128)S(1)}, s32[20]{0:T(128)S(1)}, u32[]{:S(2)}, u32[]{:S(2)}) %collective-permute-start) | collective-permute-done | bytes 112 | tf_op jit(solution)/shard_map/ppermute | solution.py:290
  16.2 1.2 %collective-permute-start.2 = (s32[20]{0:T(128)S(1)}, s32[20]{0:T(128)S(1)}, u32[]{:S(2)}, u32[]{:S(2)}) collective-permute-start(s32[20]{0:T(128)S(1)} %get-tuple-element.36), channel_id=1, source_target_pairs={{0,3},{1,0},{2,1},{3,2},{4,7},{5,4},{6,5},{7,6},{8,11},{9,8},{10,9... | collective-permute-start | bytes 248 | tf_op jit(solution)/shard_map/ppermute | solution.py:290
  17.4 2.0 %collective-permute-done.1.refs_2_ = s32[20]{0:T(128)S(1)} collective-permute-done((s32[20]{0:T(128)S(1)}, s32[20]{0:T(128)S(1)}, u32[]{:S(2)}, u32[]{:S(2)}) %collective-permute-start.1) | collective-permute-done | bytes 112 | tf_op jit(solution)/shard_map/ppermute | solution.py:290
  19.4 0.6 %collective-permute-done.2.refs_3_ = s32[20]{0:T(128)S(1)} collective-permute-done((s32[20]{0:T(128)S(1)}, s32[20]{0:T(128)S(1)}, u32[]{:S(2)}, u32[]{:S(2)}) %collective-permute-start.2) | collective-permute-done | bytes 112 | tf_op jit(solution)/shard_map/ppermute | solution.py:290
  20.0 1.2 %project.1 = (f32[9,8,128]{2,1,0:T(8,128)S(1)}, f32[9,8,128]{2,1,0:T(8,128)S(1)}, f32[9,8,128]{2,1,0:T(8,128)S(1)}, f32[9,8,128]{2,1,0:T(8,128)S(1)}) custom-call(s32[20]{0:T(128)S(1)} %get-tuple-element.33.refs_0_, s32[20]{0:T(128)S(1)} %collective-permute-done.refs_1_, s32[20]{0:T(128)S(1)} %collective-permute-done.1.refs_2_, ...), custom_call_target="tpu_custom_call" | custom-call | flops 4000000 | bytes 1000000 | tf_op jit(solution)/shard_map/project/pallas_call | solution.py:366
  21.2 2.8 %collective-permute-start.3 = (f32[9,8,128]{2,1,0:T(8,128)S(1)}, f32[9,8,128]{2,1,0:T(8,128)S(1)}, u32[]{:S(2)}, u32[]{:S(2)}) collective-permute-start(f32[9,8,128]{2,1,0:T(8,128)S(1)} %get-tuple-element.38), channel_id=1, source_target_pairs={{0,3},{1,0},{2,1},{3,2},{4,7},{5,4},{6,5},{7,6},{8,11},{9,8},{10,9... | collective-permute-start | bytes 110600 | tf_op jit(solution)/shard_map/ppermute | solution.py:290
  24.0 3.3 %collective-permute-done.8.refs_10_ = f32[4,8,128]{2,1,0:T(8,128)S(1)} collective-permute-done((f32[4,8,128]{2,1,0:T(8,128)S(1)}, f32[4,8,128]{2,1,0:T(8,128)S(1)}, u32[]{:S(2)}, u32[]{:S(2)}) %collective-permute-start.8) | collective-permute-done | bytes 16416 | tf_op jit(solution)/shard_map/ppermute | solution.py:290
  27.3 0.1 collective-permute-start.7
  27.4 1.1 %collective-permute-done.7.refs_9_ = f32[4,8,128]{2,1,0:T(8,128)S(1)} collective-permute-done((f32[4,8,128]{2,1,0:T(8,128)S(1)}, f32[4,8,128]{2,1,0:T(8,128)S(1)}, u32[]{:S(2)}, u32[]{:S(2)}) %collective-permute-start.7) | collective-permute-done | bytes 16416 | tf_op jit(solution)/shard_map/ppermute | solution.py:290
  28.4 0.8 %collective-permute-start.4 = (f32[9,8,128]{2,1,0:T(8,128)S(1)}, f32[9,8,128]{2,1,0:T(8,128)S(1)}, u32[]{:S(2)}, u32[]{:S(2)}) collective-permute-start(f32[9,8,128]{2,1,0:T(8,128)S(1)} %get-tuple-element.39), channel_id=1, source_target_pairs={{0,2},{1,3},{2,0},{3,1},{4,6},{5,7},{6,4},{7,5},{8,10},{9,11},{10,... | collective-permute-start | bytes 110600 | tf_op jit(solution)/shard_map/ppermute | solution.py:290
  29.2 0.0 collective-permute-done.3.refs_4_
  29.2 0.0 collective-permute-start.5
  29.2 4.1 %collective-permute-done.4.refs_5_ = f32[9,8,128]{2,1,0:T(8,128)S(1)} collective-permute-done((f32[9,8,128]{2,1,0:T(8,128)S(1)}, f32[9,8,128]{2,1,0:T(8,128)S(1)}, u32[]{:S(2)}, u32[]{:S(2)}) %collective-permute-start.4) | collective-permute-done | bytes 36896 | tf_op jit(solution)/shard_map/ppermute | solution.py:290
  33.3 1.7 %collective-permute-done.5.refs_6_ = f32[9,8,128]{2,1,0:T(8,128)S(1)} collective-permute-done((f32[9,8,128]{2,1,0:T(8,128)S(1)}, f32[9,8,128]{2,1,0:T(8,128)S(1)}, u32[]{:S(2)}, u32[]{:S(2)}) %collective-permute-start.5) | collective-permute-done | bytes 36896 | tf_op jit(solution)/shard_map/ppermute | solution.py:290
  35.0 0.0 collective-permute-done.10.refs_12_
  35.0 1.9 %shard_map.85 = (f32[12,8,16,128]{3,2,1,0:T(8,128)S(1)}, f32[8,16,128]{2,1,0:T(8,128)S(1)}, f32[8,16,128]{2,1,0:T(8,128)S(1)}, f32[8,16,128]{2,1,0:T(8,128)S(1)}...) custom-call(f32[12,8,16,128]{3,2,1,0:T(8,128)S(1)} %copy-done.1, ...), custom_call_target="tpu_custom_call" | custom-call | flops 8000000 | bytes 3000000 | tf_op jit(solution)/shard_map/pallas_call | solution.py:393
  36.9 0.6 %collective-permute-start.11 = (f32[2,13,8,128]{3,2,1,0:T(8,128)S(1)}, f32[2,13,8,128]{3,2,1,0:T(8,128)S(1)}, u32[]{:S(2)}, u32[]{:S(2)}) collective-permute-start(f32[2,13,8,128]{3,2,1,0:T(8,128)S(1)} %get-tuple-element.50), channel_id=1, source_target_pairs={{0,16},{16,0},{1,17},{17,1},{2,18},{18,2},{3,19},{19,3},{4,20},{20... | collective-permute-start | bytes 319496 | tf_op jit(solution)/shard_map/ppermute | solution.py:290
  37.6 0.7 %collective-permute-start.15 = (f32[13,16,128]{2,1,0:T(8,128)S(1)}, f32[13,16,128]{2,1,0:T(8,128)S(1)}, u32[]{:S(2)}, u32[]{:S(2)}) collective-permute-start(f32[13,16,128]{2,1,0:T(8,128)S(1)} %get-tuple-element.53), channel_id=1, source_target_pairs={{0,0},{1,2},{2,1},{3,3},{4,4},{5,6},{6,5},{7,7},{8,8},{9,10},{10,9... | collective-permute-start | bytes 319496 | tf_op jit(solution)/shard_map/ppermute | solution.py:290
  38.2 0.1 collective-permute-start.13
  38.3 1.5 %collective-permute-start.12 = (f32[4,8,128]{2,1,0:T(8,128)S(1)}, f32[4,8,128]{2,1,0:T(8,128)S(1)}, u32[]{:S(2)}, u32[]{:S(2)}) collective-permute-start(f32[4,8,128]{2,1,0:T(8,128)S(1)} %get-tuple-element.51), channel_id=1, source_target_pairs={{0,4},{4,0},{8,12},{12,8},{1,5},{5,1},{9,13},{13,9},{2,6},{6,2},{1... | collective-permute-start | bytes 49160 | tf_op jit(solution)/shard_map/ppermute | solution.py:290
  39.8 1.8 %collective-permute-done.13.refs_6_ = f32[4,8,128]{2,1,0:T(8,128)S(1)} collective-permute-done((f32[4,8,128]{2,1,0:T(8,128)S(1)}, f32[4,8,128]{2,1,0:T(8,128)S(1)}, u32[]{:S(2)}, u32[]{:S(2)}) %collective-permute-start.13) | collective-permute-done | bytes 16416 | tf_op jit(solution)/shard_map/ppermute | solution.py:290
  41.6 0.1 collective-permute-done.11.refs_4_
  41.7 0.5 collective-permute-done.14.refs_7_
  42.3 1.3 %shard_map.86 = (f32[12,8,16,128]{3,2,1,0:T(8,128)S(1)}, f32[8,16,128]{2,1,0:T(8,128)S(1)}, f32[8,16,128]{2,1,0:T(8,128)S(1)}, f32[2,13,8,128]{3,2,1,0:T(8,128)S...) custom-call(f32[12,8,16,128]{3,2,1,0:T(8,128)S(1)} %get-tuple-element.46.refs_0_, ...), custom_call_target="tpu_custom_call" | custom-call | flops 8000000 | bytes 3000000 | tf_op jit(solution)/shard_map/pallas_call | solution.py:393
  43.5 1.5 %collective-permute-start.16 = (f32[2,13,8,128]{3,2,1,0:T(8,128)S(1)}, f32[2,13,8,128]{3,2,1,0:T(8,128)S(1)}, u32[]{:S(2)}, u32[]{:S(2)}) collective-permute-start(f32[2,13,8,128]{3,2,1,0:T(8,128)S(1)} %get-tuple-element.57), channel_id=1, source_target_pairs={{0,16},{16,0},{1,17},{17,1},{2,18},{18,2},{3,19},{19,3},{4,20},{20... | collective-permute-start | bytes 319496 | tf_op jit(solution)/shard_map/ppermute | solution.py:290
  45.1 3.9 %collective-permute-start.19 = (f32[13,16,128]{2,1,0:T(8,128)S(1)}, f32[13,16,128]{2,1,0:T(8,128)S(1)}, u32[]{:S(2)}, u32[]{:S(2)}) collective-permute-start(f32[13,16,128]{2,1,0:T(8,128)S(1)} %get-tuple-element.59), channel_id=1, source_target_pairs={{0,1},{1,0},{2,3},{3,2},{4,5},{5,4},{6,7},{7,6},{8,9},{9,8},{10,11... | collective-permute-start | bytes 319496 | tf_op jit(solution)/shard_map/ppermute | solution.py:290
  49.0 0.7 %collective-permute-start.20 = (f32[13,16,128]{2,1,0:T(8,128)S(1)}, f32[13,16,128]{2,1,0:T(8,128)S(1)}, u32[]{:S(2)}, u32[]{:S(2)}) collective-permute-start(f32[13,16,128]{2,1,0:T(8,128)S(1)} %get-tuple-element.60), channel_id=1, source_target_pairs={{0,0},{1,2},{2,1},{3,3},{4,4},{5,6},{6,5},{7,7},{8,8},{9,10},{10,9... | collective-permute-start | bytes 319496 | tf_op jit(solution)/shard_map/ppermute | solution.py:290
  49.6 0.1 collective-permute-start.18
  49.7 1.5 %collective-permute-start.17 = (f32[4,8,128]{2,1,0:T(8,128)S(1)}, f32[4,8,128]{2,1,0:T(8,128)S(1)}, u32[]{:S(2)}, u32[]{:S(2)}) collective-permute-start(f32[4,8,128]{2,1,0:T(8,128)S(1)} %get-tuple-element.58), channel_id=1, source_target_pairs={{0,4},{4,0},{8,12},{12,8},{1,5},{5,1},{9,13},{13,9},{2,6},{6,2},{1... | collective-permute-start | bytes 49160 | tf_op jit(solution)/shard_map/ppermute | solution.py:290
  51.3 1.8 %collective-permute-done.18.refs_6_ = f32[4,8,128]{2,1,0:T(8,128)S(1)} collective-permute-done((f32[4,8,128]{2,1,0:T(8,128)S(1)}, f32[4,8,128]{2,1,0:T(8,128)S(1)}, u32[]{:S(2)}, u32[]{:S(2)}) %collective-permute-start.18) | collective-permute-done | bytes 16416 | tf_op jit(solution)/shard_map/ppermute | solution.py:290
  53.1 1.6 %shard_map.87 = (f32[12,8,16,128]{3,2,1,0:T(8,128)}, f32[8,16,128]{2,1,0:T(8,128)}, f32[8,16,128]{2,1,0:T(8,128)}) custom-call(f32[12,8,16,128]{3,2,1,0:T(8,128)S(1)} %get-tuple-element.54.refs_0_, f32[8,16,128]{2,1,0:T(8,128)S(1)} %get-tuple-element.55.refs_1_, f32[8,16,128]{2,1,0:T(8,128)S(1)} %get-tuple-element.56.refs_2_, ...), custom_call_target="tpu_custom_call" | custom-call | flops 8000000 | bytes 3000000 | tf_op jit(solution)/shard_map/pallas_call | solution.py:393
  (17 shorter events, 0.0 us)
Async XLA Ops:
  0.6 1.1 %copy-start = (f32[12,8,16,128]{3,2,1,0:T(8,128)S(1)}, f32[12,8,16,128]{3,2,1,0:T(8,128)}, u32[]{:S(2)}) copy-start(f32[12,8,16,128]{3,2,1,0:T(8,128)} %refs_0_.1) | copy-start | bytes 2359300
  1.8 0.8 %copy-start.3 = (f32[8,16,128]{2,1,0:T(8,128)S(1)}, f32[8,16,128]{2,1,0:T(8,128)}, u32[]{:S(2)}) copy-start(f32[8,16,128]{2,1,0:T(8,128)} %refs_1_.1) | copy-start | bytes 196612
  2.9 32.1 %collective-permute-start.6 = (f32[2,13,8,128]{3,2,1,0:T(8,128)S(1)}, f32[2,13,8,128]{3,2,1,0:T(8,128)S(1)}, u32[]{:S(2)}, u32[]{:S(2)}) collective-permute-start(f32[2,13,8,128]{3,2,1,0:T(8,128)S(1)} %get-tuple-element.42), channel_id=1, source_target_pairs={{0,16},{16,0},{1,17},{17,1},{2,18},{18,2},{3,19},{19,3},{4,20},{20... | collective-permute-start | bytes 319496 | tf_op jit(solution)/shard_map/ppermute | solution.py:290
  5.9 29.1 %collective-permute-start.9 = (f32[13,16,128]{2,1,0:T(8,128)S(1)}, f32[13,16,128]{2,1,0:T(8,128)S(1)}, u32[]{:S(2)}, u32[]{:S(2)}) collective-permute-start(f32[13,16,128]{2,1,0:T(8,128)S(1)} %get-tuple-element.44), channel_id=1, source_target_pairs={{0,1},{1,0},{2,3},{3,2},{4,5},{5,4},{6,7},{7,6},{8,9},{9,8},{10,11... | collective-permute-start | bytes 319496 | tf_op jit(solution)/shard_map/ppermute | solution.py:290
  7.5 27.5 %collective-permute-start.10 = (f32[13,16,128]{2,1,0:T(8,128)S(1)}, f32[13,16,128]{2,1,0:T(8,128)S(1)}, u32[]{:S(2)}, u32[]{:S(2)}) collective-permute-start(f32[13,16,128]{2,1,0:T(8,128)S(1)} %get-tuple-element.45), channel_id=1, source_target_pairs={{0,0},{1,2},{2,1},{3,3},{4,4},{5,6},{6,5},{7,7},{8,8},{9,10},{10,9... | collective-permute-start | bytes 319496 | tf_op jit(solution)/shard_map/ppermute | solution.py:290
  8.2 0.7 %copy-start.5 = (s32[1,1,1,3,20]{4,2,3,1,0:T(1,128)S(1)}, s32[1,1,1,3,20]{4,2,3,1,0:T(1,128)}, u32[]{:S(2)}) copy-start(s32[1,1,1,3,20]{4,2,3,1,0:T(1,128)} %param.11) | copy-start | bytes 724
  8.2 0.7 %copy-start.6 = (s32[1,1,1,20]{3,2,1,0:T(1,128)S(1)}, s32[1,1,1,20]{3,2,1,0:T(1,128)}, u32[]{:S(2)}) copy-start(s32[1,1,1,20]{3,2,1,0:T(1,128)} %param.10) | copy-start | bytes 244
  8.2 0.7 %copy-start.7 = (s32[1,1,1,20]{3,2,1,0:T(1,128)S(1)}, s32[1,1,1,20]{3,2,1,0:T(1,128)}, u32[]{:S(2)}) copy-start(s32[1,1,1,20]{3,2,1,0:T(1,128)} %param.9) | copy-start | bytes 244
  8.9 11.1 %copy-start.2 = (f32[1,1,1,20,4096]{4,2,3,1,0:T(1,128)S(1)}, f32[1,1,1,20,4096]{4,2,3,1,0:T(1,128)}, u32[]{:S(2)}) copy-start(f32[1,1,1,20,4096]{4,2,3,1,0:T(1,128)} %param.8) | copy-start | bytes 983044
  8.9 26.1 %copy-start.1 = (f32[12,8,16,128]{3,2,1,0:T(8,128)S(1)}, f32[12,8,16,128]{3,2,1,0:T(8,128)}, u32[]{:S(2)}) copy-start(f32[12,8,16,128]{3,2,1,0:T(8,128)} %refs_0_.1) | copy-start | bytes 2359300
  10.5 5.7 %collective-permute-start = (s32[20]{0:T(128)S(1)}, s32[20]{0:T(128)S(1)}, u32[]{:S(2)}, u32[]{:S(2)}) collective-permute-start(s32[20]{0:T(128)S(1)} %get-tuple-element.34), channel_id=1, source_target_pairs={{0,1},{1,2},{2,3},{3,0},{4,5},{5,6},{6,7},{7,4},{8,9},{9,10},{10,1... | collective-permute-start | bytes 248 | tf_op jit(solution)/shard_map/ppermute | solution.py:290
  14.9 4.5 %collective-permute-start.1 = (s32[20]{0:T(128)S(1)}, s32[20]{0:T(128)S(1)}, u32[]{:S(2)}, u32[]{:S(2)}) collective-permute-start(s32[20]{0:T(128)S(1)} %get-tuple-element.35), channel_id=1, source_target_pairs={{0,2},{1,3},{2,0},{3,1},{4,6},{5,7},{6,4},{7,5},{8,10},{9,11},{10,... | collective-permute-start | bytes 248 | tf_op jit(solution)/shard_map/ppermute | solution.py:290
  16.2 3.8 %collective-permute-start.2 = (s32[20]{0:T(128)S(1)}, s32[20]{0:T(128)S(1)}, u32[]{:S(2)}, u32[]{:S(2)}) collective-permute-start(s32[20]{0:T(128)S(1)} %get-tuple-element.36), channel_id=1, source_target_pairs={{0,3},{1,0},{2,1},{3,2},{4,7},{5,4},{6,5},{7,6},{8,11},{9,8},{10,9... | collective-permute-start | bytes 248 | tf_op jit(solution)/shard_map/ppermute | solution.py:290
  20.0 15.0 %copy-start.4 = (f32[8,16,128]{2,1,0:T(8,128)S(1)}, f32[8,16,128]{2,1,0:T(8,128)}, u32[]{:S(2)}) copy-start(f32[8,16,128]{2,1,0:T(8,128)} %refs_1_.1) | copy-start | bytes 196612
  21.2 8.0 %collective-permute-start.3 = (f32[9,8,128]{2,1,0:T(8,128)S(1)}, f32[9,8,128]{2,1,0:T(8,128)S(1)}, u32[]{:S(2)}, u32[]{:S(2)}) collective-permute-start(f32[9,8,128]{2,1,0:T(8,128)S(1)} %get-tuple-element.38), channel_id=1, source_target_pairs={{0,3},{1,0},{2,1},{3,2},{4,7},{5,4},{6,5},{7,6},{8,11},{9,8},{10,9... | collective-permute-start | bytes 110600 | tf_op jit(solution)/shard_map/ppermute | solution.py:290
  24.0 3.3 %collective-permute-start.8 = (f32[4,8,128]{2,1,0:T(8,128)S(1)}, f32[4,8,128]{2,1,0:T(8,128)S(1)}, u32[]{:S(2)}, u32[]{:S(2)}) collective-permute-start(f32[4,8,128]{2,1,0:T(8,128)S(1)} %get-tuple-element.43), channel_id=1, source_target_pairs={{0,12},{4,8},{8,4},{12,0},{1,13},{5,9},{9,5},{13,1},{2,14},{6,10},... | collective-permute-start | bytes 49160 | tf_op jit(solution)/shard_map/ppermute | solution.py:290
  27.3 1.2 %collective-permute-start.7 = (f32[4,8,128]{2,1,0:T(8,128)S(1)}, f32[4,8,128]{2,1,0:T(8,128)S(1)}, u32[]{:S(2)}, u32[]{:S(2)}) collective-permute-start(f32[4,8,128]{2,1,0:T(8,128)S(1)} %get-tuple-element.43), channel_id=1, source_target_pairs={{0,4},{4,0},{8,12},{12,8},{1,5},{5,1},{9,13},{13,9},{2,6},{6,2},{1... | collective-permute-start | bytes 49160 | tf_op jit(solution)/shard_map/ppermute | solution.py:290
  28.4 4.9 %collective-permute-start.4 = (f32[9,8,128]{2,1,0:T(8,128)S(1)}, f32[9,8,128]{2,1,0:T(8,128)S(1)}, u32[]{:S(2)}, u32[]{:S(2)}) collective-permute-start(f32[9,8,128]{2,1,0:T(8,128)S(1)} %get-tuple-element.39), channel_id=1, source_target_pairs={{0,2},{1,3},{2,0},{3,1},{4,6},{5,7},{6,4},{7,5},{8,10},{9,11},{10,... | collective-permute-start | bytes 110600 | tf_op jit(solution)/shard_map/ppermute | solution.py:290
  29.2 5.8 %collective-permute-start.5 = (f32[9,8,128]{2,1,0:T(8,128)S(1)}, f32[9,8,128]{2,1,0:T(8,128)S(1)}, u32[]{:S(2)}, u32[]{:S(2)}) collective-permute-start(f32[9,8,128]{2,1,0:T(8,128)S(1)} %get-tuple-element.40), channel_id=1, source_target_pairs={{0,1},{1,2},{2,3},{3,0},{4,5},{5,6},{6,7},{7,4},{8,9},{9,10},{10,1... | collective-permute-start | bytes 110600 | tf_op jit(solution)/shard_map/ppermute | solution.py:290
  36.9 4.8 %collective-permute-start.11 = (f32[2,13,8,128]{3,2,1,0:T(8,128)S(1)}, f32[2,13,8,128]{3,2,1,0:T(8,128)S(1)}, u32[]{:S(2)}, u32[]{:S(2)}) collective-permute-start(f32[2,13,8,128]{3,2,1,0:T(8,128)S(1)} %get-tuple-element.50), channel_id=1, source_target_pairs={{0,16},{16,0},{1,17},{17,1},{2,18},{18,2},{3,19},{19,3},{4,20},{20... | collective-permute-start | bytes 319496 | tf_op jit(solution)/shard_map/ppermute | solution.py:290
  37.5 4.7 %collective-permute-start.14 = (f32[13,16,128]{2,1,0:T(8,128)S(1)}, f32[13,16,128]{2,1,0:T(8,128)S(1)}, u32[]{:S(2)}, u32[]{:S(2)}) collective-permute-start(f32[13,16,128]{2,1,0:T(8,128)S(1)} %get-tuple-element.52), channel_id=1, source_target_pairs={{0,1},{1,0},{2,3},{3,2},{4,5},{5,4},{6,7},{7,6},{8,9},{9,8},{10,11... | collective-permute-start | bytes 319496 | tf_op jit(solution)/shard_map/ppermute | solution.py:290
  37.6 4.7 %collective-permute-start.15 = (f32[13,16,128]{2,1,0:T(8,128)S(1)}, f32[13,16,128]{2,1,0:T(8,128)S(1)}, u32[]{:S(2)}, u32[]{:S(2)}) collective-permute-start(f32[13,16,128]{2,1,0:T(8,128)S(1)} %get-tuple-element.53), channel_id=1, source_target_pairs={{0,0},{1,2},{2,1},{3,3},{4,4},{5,6},{6,5},{7,7},{8,8},{9,10},{10,9... | collective-permute-start | bytes 319496 | tf_op jit(solution)/shard_map/ppermute | solution.py:290
  38.2 3.4 %collective-permute-start.13 = (f32[4,8,128]{2,1,0:T(8,128)S(1)}, f32[4,8,128]{2,1,0:T(8,128)S(1)}, u32[]{:S(2)}, u32[]{:S(2)}) collective-permute-start(f32[4,8,128]{2,1,0:T(8,128)S(1)} %get-tuple-element.51), channel_id=1, source_target_pairs={{0,12},{4,8},{8,4},{12,0},{1,13},{5,9},{9,5},{13,1},{2,14},{6,10},... | collective-permute-start | bytes 49160 | tf_op jit(solution)/shard_map/ppermute | solution.py:290
  38.3 3.3 %collective-permute-start.12 = (f32[4,8,128]{2,1,0:T(8,128)S(1)}, f32[4,8,128]{2,1,0:T(8,128)S(1)}, u32[]{:S(2)}, u32[]{:S(2)}) collective-permute-start(f32[4,8,128]{2,1,0:T(8,128)S(1)} %get-tuple-element.51), channel_id=1, source_target_pairs={{0,4},{4,0},{8,12},{12,8},{1,5},{5,1},{9,13},{13,9},{2,6},{6,2},{1... | collective-permute-start | bytes 49160 | tf_op jit(solution)/shard_map/ppermute | solution.py:290
  43.5 9.5 %collective-permute-start.16 = (f32[2,13,8,128]{3,2,1,0:T(8,128)S(1)}, f32[2,13,8,128]{3,2,1,0:T(8,128)S(1)}, u32[]{:S(2)}, u32[]{:S(2)}) collective-permute-start(f32[2,13,8,128]{3,2,1,0:T(8,128)S(1)} %get-tuple-element.57), channel_id=1, source_target_pairs={{0,16},{16,0},{1,17},{17,1},{2,18},{18,2},{3,19},{19,3},{4,20},{20... | collective-permute-start | bytes 319496 | tf_op jit(solution)/shard_map/ppermute | solution.py:290
  45.1 8.0 %collective-permute-start.19 = (f32[13,16,128]{2,1,0:T(8,128)S(1)}, f32[13,16,128]{2,1,0:T(8,128)S(1)}, u32[]{:S(2)}, u32[]{:S(2)}) collective-permute-start(f32[13,16,128]{2,1,0:T(8,128)S(1)} %get-tuple-element.59), channel_id=1, source_target_pairs={{0,1},{1,0},{2,3},{3,2},{4,5},{5,4},{6,7},{7,6},{8,9},{9,8},{10,11... | collective-permute-start | bytes 319496 | tf_op jit(solution)/shard_map/ppermute | solution.py:290
  49.0 4.1 %collective-permute-start.20 = (f32[13,16,128]{2,1,0:T(8,128)S(1)}, f32[13,16,128]{2,1,0:T(8,128)S(1)}, u32[]{:S(2)}, u32[]{:S(2)}) collective-permute-start(f32[13,16,128]{2,1,0:T(8,128)S(1)} %get-tuple-element.60), channel_id=1, source_target_pairs={{0,0},{1,2},{2,1},{3,3},{4,4},{5,6},{6,5},{7,7},{8,8},{9,10},{10,9... | collective-permute-start | bytes 319496 | tf_op jit(solution)/shard_map/ppermute | solution.py:290
  49.6 3.4 %collective-permute-start.18 = (f32[4,8,128]{2,1,0:T(8,128)S(1)}, f32[4,8,128]{2,1,0:T(8,128)S(1)}, u32[]{:S(2)}, u32[]{:S(2)}) collective-permute-start(f32[4,8,128]{2,1,0:T(8,128)S(1)} %get-tuple-element.58), channel_id=1, source_target_pairs={{0,12},{4,8},{8,4},{12,0},{1,13},{5,9},{9,5},{13,1},{2,14},{6,10},... | collective-permute-start | bytes 49160 | tf_op jit(solution)/shard_map/ppermute | solution.py:290
  49.7 3.3 %collective-permute-start.17 = (f32[4,8,128]{2,1,0:T(8,128)S(1)}, f32[4,8,128]{2,1,0:T(8,128)S(1)}, u32[]{:S(2)}, u32[]{:S(2)}) collective-permute-start(f32[4,8,128]{2,1,0:T(8,128)S(1)} %get-tuple-element.58), channel_id=1, source_target_pairs={{0,4},{4,0},{8,12},{12,8},{1,5},{5,1},{9,13},{13,9},{2,6},{6,2},{1... | collective-permute-start | bytes 49160 | tf_op jit(solution)/shard_map/ppermute | solution.py:290
